TPU v7x, 32 devices: a whole 2x2x4 slice. The times are simulated.
32 devices in a mesh: band: 8 (over y, x, core), lev: 4 (over z).
Axes of the slice: x: 2, y: 2, z: 4, core: 2. Of those that a mesh axis runs over, the one named last changes fastest.
Arguments:
- spectral: float32 [2, 32, 640, 640], P(None, None, 'band', 'lev'), may hold values from -0.2 to 0.2
- legendre: bfloat16 [640, 640, 640], P('band', 'lev'), may hold values from -0.25 to 0.25
- wave_order: int32 [640], replicated, may hold values from 0 to 639, each once
- jacobian: bfloat16 [32, 640, 1280], P('lev', 'band'), may hold values from 0.5 to 1.5
- obs_cell: int32 [4, 8, 2048], P('lev', 'band'), may hold values from 0 to 819199
- innovation: float32 [4, 8, 2048], P('lev', 'band'), may hold values from -6 to 6
- obs_weight: float32 [4, 8, 2048], P('lev', 'band'), may hold values from 0.01 to 0.04
- inv_var: float32 [640], P('lev'), may hold values from 5 to 50
Outputs:
- model_grid: bfloat16 [32, 640, 1280], P('lev', 'band')
- gradient: float32 [2, 32, 640, 640], P(None, None, 'band', 'lev')
Inputs may be any that keep to these rules, and one draw needn't show every extreme that they name: `wave_order`: each zonal wavenumber 0 to 639 is held by exactly one slot. `obs_cell`: an index into the device's own block of the grid, flattened in order field, latitude, longitude; cells may repeat.
All inputs are finite; a program needn't handle non-finite values.
Results may differ from a plain program's by a relative error of at most 0.0062.
Values may be sent and summed in bfloat16 or wider, within the bound.
No kernel may reach another device: no remote copies, remote signals or barrier semaphores. Data moves between devices by JAX's collectives and lax.ppermute only.
A program may use at most 128 MiB of HBM per device.

v0:
```python
import math

import jax
import jax.numpy as jnp
from jax import lax
from jax.sharding import PartitionSpec as P


def fourier_table(wave_order, width):
    columns = jnp.arange(width, dtype=jnp.int32)
    phase = wave_order[:, None] * columns[None, :] % width
    angle = phase.astype(jnp.float32) * (2.0 * math.pi / width)
    factor = jnp.where(wave_order == 0, 1.0, 2.0).astype(jnp.float32)[:, None]
    return jnp.stack([factor * jnp.cos(angle), -factor * jnp.sin(angle)]).astype(jnp.bfloat16)


def shards(spectral, legendre, wave_order, jacobian, obs_cell, innovation, obs_weight, inv_var):
    slot_count = spectral.shape[2]
    degree_count = spectral.shape[3]
    own_waves = lax.dynamic_slice_in_dim(
        wave_order, lax.axis_index("band") * slot_count, slot_count
    )
    degree = lax.axis_index("lev") * degree_count + jnp.arange(degree_count, dtype=jnp.int32)
    keep = degree[None, :, None] >= own_waves[:, None, None]
    table = jnp.where(keep, legendre, jnp.zeros_like(legendre))
    spec_low = spectral.astype(jnp.bfloat16)
    fourier = fourier_table(wave_order, jacobian.shape[2])
    summed = lax.psum_scatter(
        jnp.einsum("cfsn,snl->fcsl", spec_low, table, preferred_element_type=jnp.float32),
        "lev",
        scatter_dimension=0,
        tiled=True,
    )
    by_latitude = lax.all_to_all(
        summed.astype(jnp.bfloat16), "band", split_axis=3, concat_axis=2, tiled=True
    )
    grid = lax.dot_general(
        by_latitude, fourier, (((1, 2), (0, 1)), ((), ())), preferred_element_type=jnp.float32
    )
    model_grid = (grid * jacobian).astype(jnp.bfloat16)
    cells = obs_cell.reshape(-1)
    picked = model_grid.reshape(-1)[cells].astype(jnp.float32)
    misfit = obs_weight.reshape(-1) * (picked - innovation.reshape(-1))
    grid_adj = (
        jnp.zeros((model_grid.size,), jnp.float32).at[cells].add(misfit).reshape(model_grid.shape)
    )
    force = (grid_adj * jacobian).astype(jnp.bfloat16)
    coef_adj = jnp.einsum(
        "csj,flj->fcsl", fourier, force, preferred_element_type=jnp.float32
    ).astype(jnp.bfloat16)
    by_wave = lax.all_to_all(coef_adj, "band", split_axis=2, concat_axis=3, tiled=True)
    spec_adj = jnp.einsum(
        "fcsl,snl->cfsn",
        lax.all_gather(by_wave, "lev", axis=0, tiled=True),
        table,
        preferred_element_type=jnp.float32,
    )
    gradient = spectral * inv_var[None, None, None, :] + spec_adj
    return (model_grid, gradient)


def solution(mesh):
    in_specs = (
        P(None, None, "band", "lev"),
        P("band", "lev", None),
        P(),
        P("lev", "band", None),
        P("lev", "band", None),
        P("lev", "band", None),
        P("lev", "band", None),
        P("lev"),
    )
    out_specs = (P("lev", "band", None), P(None, None, "band", "lev"))
    return jax.shard_map(shards, mesh=mesh, in_specs=in_specs, out_specs=out_specs, check_vma=False)
```

profile of v0, /device:TPU:0, one launch (start us, length us, event | category | flops | bytes accessed | tf_op | source)
XLA Modules:
  0.0 530.7 jit_solution(14809128090837592161)
XLA Ops:
  7.2 2.8 convert_element_type.40
  10.0 1.0 copy.27
  11.2 11.4 %fusion.2 = f32[80,640,64]{1,2,0} fusion(bf16[80,160,64]{1,2,0:T(8,128)(2,1)S(1)} %bitcast.64, bf16[80,160,640]{2,1,0:T(8,128)(2,1)} %param.9, pred[80,160]{1,0:T(8,128)(4,1)S(1)} %broadcast_compare_fusion), kind=kOutput, calls=%fused_computation.5 | convolution fusion | flops 1056768000 | bytes 31142400
  22.6 223.2 %reduce-scatter.2.cloned.1.call-done = f32[8,2,80,640]{3,0,1,2:T(8,128)} async-done(((f32[32,2,80,640]{3,0,1,2:T(8,128)}), f32[8,2,80,640]{3,0,1,2:T(8,128)}) %reduce-scatter.2.cloned.1.call-update) | async-done | bytes 3276816 | tf_op jit(solution)/shard_map/reduce_scatter | solution.py:28
  245.9 2.1 convert_element_type.41
  248.0 3.5 copy.28
  251.5 3.8 all-to-all-start
  255.6 15.9 %multiply_convert_fusion.1 = (bf16[1,640,1280]{2,1,0:T(8,128)(2,1)}, bf16[1,640,1280]{2,1,0:T(8,128)(2,1)}) fusion(s32[640]{0:T(1024)S(1)} %copy-done.2, f32[640]{0:T(1024)S(1)} %get-tuple-element.12, f32[640]{0:T(1024)S(1)} %get-tuple-element.13), kind=kLoop, calls=%fused_computation.19 | loop fusion | flops 10649600 | bytes 3284480 | tf_op jit(solution)/shard_map/convert
  271.5 16.0 %all-to-all-done = bf16[8,2,80,640]{2,0,1,3:T(8,128)(2,1)S(1)} async-done(((bf16[8,2,80,640]{2,0,1,3:T(8,128)(2,1)}), bf16[8,2,80,640]{2,0,1,3:T(8,128)(2,1)S(1)}, u32[]{:S(2)}, u32[]{:S(2)}) %all-to-all-start) | async-done | bytes 1638432 | tf_op jit(solution)/shard_map/all_to_all | solution.py:34
  287.5 3.2 copy.43
  290.7 4.9 all_to_all.29
  295.6 4.7 fusion.11
  300.3 1.9 reshape.208
  302.2 13.1 %gather_fusion = bf16[2048]{0:T(1024)(128)(2,1)S(1)} fusion(bf16[819200]{0:T(1024)(128)(2,1)S(1)} %reshape.208, s32[2048]{0:T(1024)S(1)} %broadcast_clamp_fusion), kind=kCustom, calls=%fused_computation | custom fusion | bytes 16384 | tf_op jit(solution)/shard_map/gather | solution.py:42
  315.4 12.0 %scatter_custom_fusion = f32[819200]{0:T(1024)S(1)} fusion(s32[2048]{0:T(1024)S(1)} %bitcast.70, f32[2048]{0:T(1024)S(1)} %subtract_multiply_fusion, f32[]{:T(128)} %constant.40.clone.1), kind=kCustom, calls=%fused_computation.30 | custom fusion | flops 2048 | bytes 3276804 | tf_op jit(solution)/shard_map/scatter-add | solution.py:45
  327.4 2.0 reshape.210
  329.4 6.9 %fusion.20 = bf16[8,2,640,80]{2,3,1,0:T(8,128)(2,1)} fusion(bf16[1,640,1280]{2,1,0:T(8,128)(2,1)} %get-tuple-element.11, bf16[1,640,1280]{2,1,0:T(8,128)(2,1)} %get-tuple-element.10, f32[8,80,1280]{2,1,0:T(8,128)} %reshape.210, bf16[8,80,1280]{2,1,0:T(8,128)(2,1)} %param.11), kind=kOutput, calls=%fused_computation.32 | convolution fusion | flops 2106982400 | bytes 9830400 | tf_op jit(solution)/shard_map/csj,flj->fcsl/dot_general | solution.py:48
  336.3 5.8 %copy.31 = bf16[8,2,640,80]{3,1,0,2:T(2,128)(2,1)S(1)} copy(bf16[8,2,640,80]{2,3,1,0:T(8,128)(2,1)} %fusion.20) | data formatting | bytes 3276800 | tf_op jit(solution)/shard_map/convert_element_type | solution.py:50
  342.1 34.6 %all_to_all.36 = bf16[8,2,640,80]{3,1,0,2:T(2,128)(2,1)S(1)} all-to-all(bf16[8,2,640,80]{3,1,0,2:T(2,128)(2,1)S(1)} %copy.31), channel_id=1, replica_groups=mesh['band'=8,'lev'=4] {'band'}, dimensions={2} | all-to-all | bytes 3276800 | tf_op jit(solution)/shard_map/all_to_all | solution.py:51
  376.8 3.0 copy.42
  379.8 3.0 all_to_all.33
  382.8 119.0 %all-gather.2.cloned.1.call-done = bf16[32,2,80,640]{3,0,1,2:T(8,128)(2,1)} async-done(((bf16[8,2,80,640]{3,0,1,2:T(8,128)(2,1)}), bf16[32,2,80,640]{3,0,1,2:T(8,128)(2,1)}) %all-gather.2.cloned.1.call-update) | async-done | bytes 6553616 | tf_op jit(solution)/shard_map/all_gather | solution.py:54
  501.8 14.1 %bitcast_add_fusion = f32[2,32,80,160]{3,1,0,2:T(8,128)} fusion(f32[2,32,80,160]{3,2,1,0:T(8,128)} %param.8, f32[160]{0:T(256)S(1)} %copy-done.6, bf16[32,2,80,640]{3,0,1,2:T(8,128)(2,1)} %all-gather.2.cloned.1.call-done, bf16[80,160,640]{2,1,0:T(8,128)(2,1)} %param.9, pred[80,160]{1,0:T(8,128)(4,1)S(1)} %broadcast_compare_fusion), kind=kOutput, calls=%fused_computation.8 | convolution fusion | flops 1058406400 | bytes 29504640 | tf_op jit(solution)/shard_map/fcsl,snl->cfsn/dot_general | solution.py:52
  515.9 7.9 %copy.33 = f32[2,32,80,160]{3,2,1,0:T(8,128)} copy(f32[2,32,80,160]{3,1,0,2:T(8,128)} %bitcast_add_fusion) | data formatting | bytes 6553600
  (25 shorter events, 0.5 us)
Async XLA Ops:
  7.2 238.7 %reduce-scatter.2.cloned.1.call-start = ((), (), s32[]{:S(2)}) async-start(), calls=%async_computation.3 | async-start | bytes 16384000 | tf_op jit(solution)/shard_map/reduce_scatter | solution.py:28
  10.0 1.0 copy-start.2
  251.5 4.0 copy-start.5
  251.5 36.0 %all-to-all-start = ((bf16[8,2,80,640]{2,0,1,3:T(8,128)(2,1)}), bf16[8,2,80,640]{2,0,1,3:T(8,128)(2,1)S(1)}, u32[]{:S(2)}, u32[]{:S(2)}) async-start(bf16[8,2,80,640]{2,0,1,3:T(8,128)(2,1)} %copy.28), calls=%async_computation.1 | async-start | bytes 5242880 | tf_op jit(solution)/shard_map/all_to_all | solution.py:34
  255.3 246.6 %all-gather.2.cloned.1.call-start = ((), (), s32[]{:S(2)}) async-start(), calls=%async_computation.4 | async-start | bytes 8192000 | tf_op jit(solution)/shard_map/all_gather | solution.py:54
  290.7 4.9 copy-start.1
  300.3 15.0 %copy-start = (bf16[8,80,1280]{2,1,0:T(8,128)(2,1)}, bf16[8,80,1280]{2,1,0:T(8,128)(2,1)S(1)}, u32[]{:S(2)}) copy-start(bf16[8,80,1280]{2,1,0:T(8,128)(2,1)S(1)} %fusion.11) | copy-start | bytes 4915204
  300.3 15.0 %copy-start.3 = (f32[1,1,2048]{2,1,0:T(1,128)S(1)}, f32[1,1,2048]{2,1,0:T(1,128)}, u32[]{:S(2)}) copy-start(f32[1,1,2048]{2,1,0:T(1,128)} %param.14) | copy-start | bytes 24580
  300.3 15.0 %copy-start.4 = (f32[1,1,2048]{2,1,0:T(1,128)S(1)}, f32[1,1,2048]{2,1,0:T(1,128)}, u32[]{:S(2)}) copy-start(f32[1,1,2048]{2,1,0:T(1,128)} %param.13) | copy-start | bytes 24580
  379.8 122.0 %copy-start.6 = (f32[160]{0:T(256)S(1)}, f32[160]{0:T(256)}, u32[]{:S(2)}) copy-start(f32[160]{0:T(256)} %param.15) | copy-start | bytes 1924
Sparse Core Ops, SparseCore 0:
  22.7 223.0 reduce-scatter.1
  383.0 118.8 all-gather.1
where the time goes:
time: 531 us
  waiting for transfers between devices  358 us (67%)
  local copies, waits for them, and re-layouts  49.4 us (9%)
  matrix products  37.1 us (7%)
  blocking collectives  34.6 us (7%)
  other arithmetic  32.9 us (6%)
  between operations  14.2 us (3%)
    reduce_scatter x1, waiting for transfers between devices, shards(): lax.psum_scatter(jnp.einsum('cfsn,snl->fcsl', spec_low, table, preferred_...  223 us
    all_gather x1, waiting for transfers between devices, shards(): lax.all_gather(by_wave, 'lev', axis=0, tiled=True)  119 us
    all_to_all x1, blocking collectives, shards(): lax.all_to_all(coef_adj, 'band', split_axis=2, concat_axis=3, tiled=True)  34.6 us
    all_to_all x1, waiting for transfers between devices, shards(): lax.all_to_all(summed.astype(jnp.bfloat16), 'band', split_axis=3, concat_...  16 us
    another operation x1, other arithmetic  15.9 us
    dot_general x1, matrix products, shards(): jnp.einsum('fcsl,snl->cfsn', lax.all_gather(by_wave, 'lev', axis=0, tiled...  14.1 us
    gather x1, local copies, waits for them, and re-layouts, shards(): picked = model_grid.reshape(-1)[cells].astype(jnp.float32)  13.1 us
    scatter-add x1, other arithmetic, shards(): jnp.zeros((model_grid.size,), jnp.float32).at[cells].add(misfit)  12 us
  transfers between devices with their start and end apart: 3, of which 3 were waited for; matrix products, arithmetic and copies ran while one was open for 3% of the time, Pallas kernels for 0%

commit v1 on v0

--- a/solution.py
+++ b/solution.py
@@ -1,9 +1,17 @@
+import functools
 import math
 
 import jax
 import jax.numpy as jnp
 from jax import lax
+from jax.experimental import pallas as pl
+from jax.experimental.pallas import tpu as pltpu
 from jax.sharding import PartitionSpec as P
+
+S_CHUNK = 16
+O_CHUNK = 256
+LOW = 32
+SPARSE_BYTES = 48 * 2**20
 
 
 def fourier_table(wave_order, width):
@@ -14,7 +22,320 @@
     return jnp.stack([factor * jnp.cos(angle), -factor * jnp.sin(angle)]).astype(jnp.bfloat16)
 
 
-def shards(spectral, legendre, wave_order, jacobian, obs_cell, innovation, obs_weight, inv_var):
+def lane_tiles(width):
+    return [(t, t * 128, min(width, (t + 1) * 128)) for t in range(-(-width // 128))]
+
+
+def put_rows(ref, value):
+    for t, lo, hi in lane_tiles(value.shape[1]):
+        ref[t, :, : hi - lo] = value[:, lo:hi]
+
+
+def get_rows(ref, at, width):
+    pieces = [ref[t, at, :][:, : hi - lo] for t, lo, hi in lane_tiles(width)]
+    return pieces[0] if len(pieces) == 1 else jnp.concatenate(pieces, axis=1)
+
+
+def put_strided(ref, at, value):
+    width = value.shape[1]
+    for t, lo, hi in lane_tiles(width):
+        piece = value[:, lo:hi]
+        if hi - lo < 128:
+            piece = jnp.concatenate(
+                [piece, jnp.zeros((piece.shape[0], 128 - hi + lo), piece.dtype)], axis=1
+            )
+        ref[t, at, :] = piece
+
+
+def synth_kernel(thr_ref, spec_ref, table_ref, out_ref, spec_s, coef_s, row_s):
+    parts, bands = out_ref.shape[0], out_ref.shape[1]
+    cf, sc, deg = spec_ref.shape
+    lats = table_ref.shape[2]
+    f_own = cf // 2 // parts
+    l_own = lats // bands
+    put_rows(spec_s, spec_ref[...].reshape(cf * sc, deg))
+    degree = lax.broadcasted_iota(jnp.int32, (cf, deg), 1)
+    base = pl.program_id(0) * sc
+    for s in range(sc):
+        a = get_rows(spec_s, pl.ds(s, cf, stride=sc), deg)
+        a = jnp.where(degree >= thr_ref[base + s], a, 0.0).astype(jnp.bfloat16)
+        put_strided(
+            coef_s,
+            pl.ds(s, cf, stride=sc),
+            jnp.dot(a, table_ref[s], preferred_element_type=jnp.float32),
+        )
+
+    def regroup(i, carry):
+        k = i // 2
+        c = i % 2
+        for f in range(f_own):
+            start = pl.multiple_of(((c * parts + k) * f_own + f) * sc, sc)
+            x = get_rows(coef_s, pl.ds(start, sc), lats)
+            for b in range(bands):
+                row_s[b, :, f * l_own : (f + 1) * l_own] = x[:, b * l_own : (b + 1) * l_own]
+        for b in range(bands):
+            out_ref[k, b, c, :, :] = row_s[b].astype(jnp.bfloat16)
+        return carry
+
+    lax.fori_loop(0, 2 * parts, regroup, 0)
+
+
+def synth(thr, spec, table, parts, bands):
+    cf, slots, deg = spec.shape
+    lats = table.shape[2]
+    f_own = cf // 2 // parts
+    l_own = lats // bands
+    sc = S_CHUNK
+    return pl.pallas_call(
+        synth_kernel,
+        grid_spec=pltpu.PrefetchScalarGridSpec(
+            num_scalar_prefetch=1,
+            grid=(slots // sc,),
+            in_specs=[
+                pl.BlockSpec((cf, sc, deg), lambda i, t: (0, i, 0)),
+                pl.BlockSpec((sc, deg, lats), lambda i, t: (i, 0, 0)),
+            ],
+            out_specs=pl.BlockSpec(
+                (parts, bands, 2, sc, f_own * l_own), lambda i, t: (0, 0, 0, i, 0)
+            ),
+            scratch_shapes=[
+                pltpu.VMEM((-(-deg // 128), cf * sc, 128), jnp.float32),
+                pltpu.VMEM((-(-lats // 128), cf * sc, 128), jnp.float32),
+                pltpu.VMEM((bands, sc, f_own * l_own), jnp.float32),
+            ],
+        ),
+        out_shape=jax.ShapeDtypeStruct((parts, bands, 2, slots, f_own * l_own), jnp.bfloat16),
+        compiler_params=pltpu.CompilerParams(
+            dimension_semantics=("arbitrary",), vmem_limit_bytes=40 * 2**20
+        ),
+        name="synth",
+    )(thr, spec, table)
+
+
+def pick_kernel(coef_ref, row_ref, high_ref, low_ref, tab_ref, g_ref, p_ref):
+    cs, rows = coef_ref.shape[1], coef_ref.shape[2]
+    slots = cs // 2
+    obs = row_ref.shape[2]
+    highs = (tab_ref.shape[1] - 2 * LOW) // 2
+    row_id = lax.broadcasted_iota(jnp.int32, (rows, O_CHUNK), 0)
+    high_id = lax.broadcasted_iota(jnp.int32, (highs, O_CHUNK), 0)
+    low_id = lax.broadcasted_iota(jnp.int32, (LOW, O_CHUNK), 0)
+    for o in range(obs // O_CHUNK):
+        at = slice(o * O_CHUNK, (o + 1) * O_CHUNK)
+        a = (high_id == high_ref[0, :, at]).astype(jnp.float32)
+        b = (low_id == low_ref[0, :, at]).astype(jnp.float32)
+        hot = jnp.concatenate([a, a, b, b], axis=0).astype(jnp.bfloat16)
+        parts = jnp.dot(tab_ref[...], hot, preferred_element_type=jnp.float32)
+        uc, us = parts[:slots], parts[slots : 2 * slots]
+        vc, vs = parts[2 * slots : 3 * slots], parts[3 * slots :]
+        gc = (uc * vc - us * vs).astype(jnp.bfloat16)
+        gs = (-(us * vc + uc * vs)).astype(jnp.bfloat16)
+        g_ref[0, :slots, at] = gc
+        g_ref[0, slots:, at] = gs
+        pick = (row_id == row_ref[0, :, at]).astype(jnp.float32).astype(jnp.bfloat16)
+        t = jnp.dot(coef_ref[0], pick, preferred_element_type=jnp.float32)
+        p = t[:slots] * gc.astype(jnp.float32) + t[slots:] * gs.astype(jnp.float32)
+        p_ref[0, :, at] = jnp.sum(p, axis=0, keepdims=True)
+
+
+def pick(coef, row, high, low, tab):
+    blocks, cs, rows = coef.shape
+    obs = row.shape[2]
+    one = pl.BlockSpec((1, 1, obs), lambda i: (i, 0, 0))
+    return pl.pallas_call(
+        pick_kernel,
+        grid=(blocks,),
+        in_specs=[
+            pl.BlockSpec((1, cs, rows), lambda i: (i, 0, 0)),
+            one,
+            one,
+            one,
+            pl.BlockSpec(tab.shape, lambda i: (0, 0)),
+        ],
+        out_specs=[pl.BlockSpec((1, cs, obs), lambda i: (i, 0, 0)), one],
+        out_shape=[
+            jax.ShapeDtypeStruct((blocks, cs, obs), jnp.bfloat16),
+            jax.ShapeDtypeStruct((blocks, 1, obs), jnp.float32),
+        ],
+        compiler_params=pltpu.CompilerParams(
+            dimension_semantics=("arbitrary",), vmem_limit_bytes=40 * 2**20
+        ),
+        name="pick",
+    )(coef, row, high, low, tab)
+
+
+def spread_kernel(g_ref, row_ref, val_ref, out_ref, hot_s, coef_s, *, bands):
+    cs, obs = g_ref.shape[1], g_ref.shape[2]
+    slots = cs // 2
+    f_own = out_ref.shape[1]
+    lats = out_ref.shape[3]
+    l_own = lats // bands
+    rows = f_own * l_own
+    row_id = lax.broadcasted_iota(jnp.int32, (rows, O_CHUNK), 0)
+    for o in range(obs // O_CHUNK):
+        at = slice(o * O_CHUNK, (o + 1) * O_CHUNK)
+        hot_s[:, at] = jnp.where(row_id == row_ref[0, :, at], val_ref[0, :, at], 0.0).astype(
+            jnp.bfloat16
+        )
+    acc = lax.dot_general(
+        hot_s[...], g_ref[0], (((1,), (1,)), ((), ())), preferred_element_type=jnp.float32
+    )
+    b = pl.program_id(1)
+    start = pl.multiple_of(b * l_own, 8)
+    for f in range(f_own):
+        coef_s[f, pl.ds(start, l_own), :] = acc[f * l_own : (f + 1) * l_own]
+
+    @pl.when(b == bands - 1)
+    def _():
+        for f in range(f_own):
+            t = coef_s[f].T.astype(jnp.bfloat16)
+            out_ref[0, f] = t[:slots]
+            out_ref[1, f] = t[slots:]
+
+
+def spread(g, row, val, parts, bands, fields, lats):
+    blocks, cs, obs = g.shape
+    f_own = fields // parts
+    l_own = lats // bands
+    one = pl.BlockSpec((1, 1, obs), lambda k, b: (k * bands + b, 0, 0))
+    return pl.pallas_call(
+        functools.partial(spread_kernel, bands=bands),
+        grid=(parts, bands),
+        in_specs=[pl.BlockSpec((1, cs, obs), lambda k, b: (k * bands + b, 0, 0)), one, one],
+        out_specs=pl.BlockSpec((2, f_own, cs // 2, lats), lambda k, b: (0, k, 0, 0)),
+        out_shape=jax.ShapeDtypeStruct((2, fields, cs // 2, lats), jnp.bfloat16),
+        scratch_shapes=[
+            pltpu.VMEM((f_own * l_own, obs), jnp.bfloat16),
+            pltpu.VMEM((f_own, lats, cs), jnp.float32),
+        ],
+        compiler_params=pltpu.CompilerParams(
+            dimension_semantics=("arbitrary", "arbitrary"), vmem_limit_bytes=40 * 2**20
+        ),
+        name="spread",
+    )(g, row, val)
+
+
+def analyse_kernel(thr_ref, coef_ref, table_ref, spec_ref, inv_ref, out_ref, coef_s, out_s):
+    cf, sc, lats = coef_ref.shape
+    deg = spec_ref.shape[2]
+    put_rows(coef_s, coef_ref[...].astype(jnp.float32).reshape(cf * sc, lats))
+    degree = lax.broadcasted_iota(jnp.int32, (cf, deg), 1)
+    base = pl.program_id(0) * sc
+    for s in range(sc):
+        a = get_rows(coef_s, pl.ds(s, cf, stride=sc), lats).astype(jnp.bfloat16)
+        o = lax.dot_general(
+            a, table_ref[s], (((1,), (1,)), ((), ())), preferred_element_type=jnp.float32
+        )
+        put_strided(
+            out_s, pl.ds(s, cf, stride=sc), jnp.where(degree >= thr_ref[base + s], o, 0.0)
+        )
+    adj = get_rows(out_s, slice(None), deg).reshape(cf, sc, deg)
+    out_ref[...] = spec_ref[...] * inv_ref[...][None] + adj
+
+
+def analyse(thr, coef, table, spec, inv_var):
+    cf, slots, lats = coef.shape
+    deg = spec.shape[2]
+    sc = S_CHUNK
+    return pl.pallas_call(
+        analyse_kernel,
+        grid_spec=pltpu.PrefetchScalarGridSpec(
+            num_scalar_prefetch=1,
+            grid=(slots // sc,),
+            in_specs=[
+                pl.BlockSpec((cf, sc, lats), lambda i, t: (0, i, 0)),
+                pl.BlockSpec((sc, deg, lats), lambda i, t: (i, 0, 0)),
+                pl.BlockSpec((cf, sc, deg), lambda i, t: (0, i, 0)),
+                pl.BlockSpec((1, deg), lambda i, t: (0, 0)),
+            ],
+            out_specs=pl.BlockSpec((cf, sc, deg), lambda i, t: (0, i, 0)),
+            scratch_shapes=[
+                pltpu.VMEM((-(-lats // 128), cf * sc, 128), jnp.float32),
+                pltpu.VMEM((-(-deg // 128), cf * sc, 128), jnp.float32),
+            ],
+        ),
+        out_shape=jax.ShapeDtypeStruct((cf, slots, deg), jnp.float32),
+        compiler_params=pltpu.CompilerParams(
+            dimension_semantics=("arbitrary",), vmem_limit_bytes=40 * 2**20
+        ),
+        name="analyse",
+    )(thr, coef, table, spec, inv_var)
+
+
+def observation_table(waves, width):
+    highs = width // LOW
+    factor = jnp.where(waves == 0, 1.0, 2.0).astype(jnp.float32)[:, None]
+
+    def pair(columns, scale):
+        phase = waves[:, None] * columns[None, :] % width
+        angle = phase.astype(jnp.float32) * (2.0 * math.pi / width)
+        exact = jnp.concatenate([scale * jnp.cos(angle), scale * jnp.sin(angle)], axis=0)
+        near = exact.astype(jnp.bfloat16)
+        rest = (exact - near.astype(jnp.float32)).astype(jnp.bfloat16)
+        return jnp.concatenate([near, rest], axis=1)
+
+    u = pair(LOW * jnp.arange(highs, dtype=jnp.int32), factor)
+    v = pair(jnp.arange(LOW, dtype=jnp.int32), 1.0)
+    top = jnp.concatenate([u, jnp.zeros((u.shape[0], v.shape[1]), u.dtype)], axis=1)
+    bottom = jnp.concatenate([jnp.zeros((v.shape[0], u.shape[1]), u.dtype), v], axis=1)
+    return jnp.concatenate([top, bottom], axis=0)
+
+
+def sparse_shards(parts, bands, spectral, legendre, wave_order, jacobian, obs_cell, innovation, obs_weight, inv_var):
+    _, fields, slots, degrees = spectral.shape
+    lats = legendre.shape[2]
+    f_own, l_own, width = jacobian.shape
+    obs = obs_cell.shape[-1]
+    own_waves = lax.dynamic_slice_in_dim(wave_order, lax.axis_index("band") * slots, slots)
+    thr = own_waves - lax.axis_index("lev") * degrees
+    spec = spectral.reshape(2 * fields, slots, degrees)
+
+    partial = synth(thr, spec, legendre, parts, bands)
+    summed = lax.psum_scatter(
+        partial.reshape(parts, bands * 2 * slots, f_own * l_own), "lev", scatter_dimension=0, tiled=True
+    )
+
+    cells = obs_cell.reshape(1, 1, obs)
+    all_cells = lax.all_gather(cells, ("lev", "band"), axis=0, tiled=True)
+    row = all_cells // width
+    lon = all_cells % width
+    g, p = pick(
+        partial.reshape(parts * bands, 2 * slots, f_own * l_own),
+        row,
+        lon // LOW,
+        lon % LOW,
+        observation_table(own_waves, width),
+    )
+    at_owner = lax.all_to_all(p, ("lev", "band"), split_axis=0, concat_axis=0, tiled=True)
+    grid_at = jnp.sum(at_owner.reshape(parts * bands, obs), axis=0)
+    jac_at = jacobian.reshape(-1)[obs_cell.reshape(-1)].astype(jnp.float32)
+    misfit = obs_weight.reshape(-1) * (grid_at * jac_at - innovation.reshape(-1))
+    val = lax.all_gather((misfit * jac_at).reshape(1, 1, obs), ("lev", "band"), axis=0, tiled=True)
+    coef_adj = spread(g, row, val, parts, bands, fields, lats)
+    gradient = analyse(
+        thr,
+        coef_adj.reshape(2 * fields, slots, lats),
+        legendre,
+        spec,
+        inv_var.reshape(1, degrees),
+    ).reshape(spectral.shape)
+
+    by_latitude = lax.all_to_all(
+        summed.reshape(bands, 2 * slots, f_own * l_own), "band", split_axis=0, concat_axis=0, tiled=True
+    )
+    fourier = fourier_table(wave_order, width).reshape(2, bands, slots, width)
+    fourier = fourier.transpose(1, 0, 2, 3).reshape(bands * 2 * slots, width)
+    grid = lax.dot_general(
+        by_latitude.reshape(bands * 2 * slots, f_own * l_own),
+        fourier,
+        (((0,), (0,)), ((), ())),
+        preferred_element_type=jnp.float32,
+    )
+    model_grid = (grid * jacobian.reshape(f_own * l_own, width)).astype(jnp.bfloat16)
+    return model_grid.reshape(jacobian.shape), gradient
+
+
+def dense_shards(spectral, legendre, wave_order, jacobian, obs_cell, innovation, obs_weight, inv_var):
     slot_count = spectral.shape[2]
     degree_count = spectral.shape[3]
     own_waves = lax.dynamic_slice_in_dim(
@@ -60,6 +381,23 @@
 
 
 def solution(mesh):
+    parts, bands = mesh.shape["lev"], mesh.shape["band"]
+
+    def shards(spectral, legendre, wave_order, jacobian, obs_cell, innovation, obs_weight, inv_var):
+        slots = spectral.shape[2]
+        l_own, width = jacobian.shape[1:]
+        obs = obs_cell.shape[-1]
+        table_bytes = parts * bands * obs * 4 * slots
+        fits = (
+            table_bytes <= SPARSE_BYTES
+            and slots % S_CHUNK == 0
+            and l_own % 16 == 0
+            and obs % O_CHUNK == 0
+            and width % LOW == 0
+        )
+        args = (spectral, legendre, wave_order, jacobian, obs_cell, innovation, obs_weight, inv_var)
+        return sparse_shards(parts, bands, *args) if fits else dense_shards(*args)
+
     in_specs = (
         P(None, None, "band", "lev"),
         P("band", "lev", None),

time: 531 us -> 287 us (0.54)
  waiting for transfers between devices: 358 us -> 6.5 us
  Pallas kernels: 0 us -> 115 us
  blocking collectives: 34.6 us -> 88.5 us
  matrix products: 37.1 us -> 5.45 us
  local copies, waits for them, and re-layouts: 49.4 us -> 24.7 us
  other arithmetic: 32.9 us -> 23.1 us
    reduce_scatter x1, waiting for transfers between devices: 223 us -> 6.47 us  [sparse_shards(): lax.psum_scatter(partial.reshape(parts, bands * 2 * slots, f_own * l_own)...]
    all_gather x1 -> x0, waiting for transfers between devices: 119 us -> none  [shards(): lax.all_gather(by_wave, 'lev', axis=0, tiled=True)]
    pallas_call x0 -> x4, Pallas kernels: none -> 115 us  [the longest x1 42.3 us: pick(): pl.pallas_call(pick_kernel, grid=(blocks,), in_specs=[pl.BlockSpec((1, cs...]
    all_gather x0 -> x2, blocking collectives: none -> 88.5 us  [the longest x1 46.3 us: sparse_shards(): all_cells = lax.all_gather(cells, ('lev', 'band'), axis=0, tiled=True)]
    all_to_all x1 -> x0, blocking collectives: 34.6 us -> none  [shards(): lax.all_to_all(coef_adj, 'band', split_axis=2, concat_axis=3, tiled=True)]
    dot_general x3 -> x1, matrix products: 25.7 us -> 5.45 us  [sparse_shards(): lax.dot_general(by_latitude.reshape(bands * 2 * slots, f_own * l_own), fo...]
    all_to_all x1 -> x2, waiting for transfers between devices: 16 us -> 0.01 us  [the longest x1 0.01 us: sparse_shards(): lax.all_to_all(p, ('lev', 'band'), split_axis=0, concat_axis=0, tiled=True)]
    all_to_all x4 -> x0, local copies, waits for them, and re-layouts: 14.1 us -> none  [the longest x2 8.09 us: shards(): lax.all_to_all(summed.astype(jnp.bfloat16), 'band', split_axis=3, concat_...]
  transfers between devices with their start and end apart: 3 -> 3, of which waited for: 3 -> 1; matrix products, arithmetic and copies ran while one was open for 3% -> 14% of each run, Pallas kernels for 0% -> 32%
where the time goes in v1:
time: 287 us; the launch traced here: 286 us
  Pallas kernels  115 us (40%)
  blocking collectives  88.5 us (31%)
  local copies, waits for them, and re-layouts  24.7 us (9%)
  other arithmetic  23.1 us (8%)
  between operations  14.3 us (5%)
  starting transfers between devices  7.66 us (3%)
  waiting for transfers between devices  6.5 us (2%)
  matrix products  5.45 us (2%)
    all_gather x1, blocking collectives, sparse_shards(): all_cells = lax.all_gather(cells, ('lev', 'band'), axis=0, tiled=True)  46.3 us
    pallas_call x1, Pallas kernels, pick(): pl.pallas_call(pick_kernel, grid=(blocks,), in_specs=[pl.BlockSpec((1, cs...  42.3 us
    all_gather x1, blocking collectives, sparse_shards(): lax.all_gather((misfit * jac_at).reshape(1, 1, obs), ('lev', 'band'), axi...  42.2 us
    pallas_call x1, Pallas kernels, spread(): pl.pallas_call(functools.partial(spread_kernel, bands=bands), grid=(parts...  36.1 us
    pallas_call x1, Pallas kernels, synth(): pl.pallas_call(synth_kernel, grid_spec=pltpu.PrefetchScalarGridSpec(num_s...  23.4 us
    another operation x1, other arithmetic  15.2 us
    pallas_call x1, Pallas kernels, analyse(): pl.pallas_call(analyse_kernel, grid_spec=pltpu.PrefetchScalarGridSpec(num...  13.5 us
    gather x1, local copies, waits for them, and re-layouts, sparse_shards(): jac_at = jacobian.reshape(-1)[obs_cell.reshape(-1)].astype(jnp.float32)  13.1 us
  transfers between devices with their start and end apart: 3, of which 1 were waited for; matrix products, arithmetic and copies ran while one was open for 14% of the time, Pallas kernels for 32%

profile of v1, /device:TPU:0, one launch (start us, length us, event | category | flops | bytes accessed | tf_op | source)
XLA Modules:
  0.0 285.7 jit_solution(14940625848189968637)
XLA Ops:
  7.2 0.8 compare_select_fusion.5
  8.0 2.5 copy-done.2
  10.5 23.4 %synth.1 = bf16[4,8,2,80,640]{4,3,2,1,0:T(8,128)(2,1)S(1)} custom-call(s32[80]{0:T(128)S(1)} %broadcast_subtract_fusion.thr_ref, f32[64,80,160]{2,1,0:T(8,128)S(1)} %bitcast.24, bf16[80,160,640]{2,1,0:T(8,128)(2,1)} %table_ref.3), custom_call_target="tpu_custom_call" | custom-call | tf_op jit(solution)/shard_map/synth/pallas_call | solution.py:89
  33.9 2.8 copy-done
  37.7 46.3 %all_gather.6 = s32[32,1,2048]{2,1,0:T(1,128)S(1)} all-gather(s32[1,1,2048]{2,1,0:T(1,128)S(1)} %copy-done.5), channel_id=1, replica_groups=mesh['band'=8,'lev'=4] {'lev','band'}, dimensions={0}, use_global_device_ids=true | all-gather | bytes 270336 | tf_op jit(solution)/shard_map/all_gather | solution.py:299
  84.0 2.8 and_select_fusion
  86.8 0.9 and_select_fusion.1.high_ref
  87.8 2.9 copy-done.1
  90.6 42.3 %pick.1 = (bf16[32,160,2048]{2,1,0:T(8,128)(2,1)}, f32[32,1,2048]{2,1,0:T(1,128)}) custom-call(bf16[32,160,640]{2,1,0:T(8,128)(2,1)S(1)} %bitcast.22, s32[32,1,2048]{2,1,0:T(1,128)S(1)} %get-tuple-element.11.row_ref, s32[32,1,2048]{2,1,0:T(1,128)S(1)} %and_select_fusion.1.high_ref, s32[32,1,2048]{2,1,0:T(1,128)S(1)} %get-tuple-element.8.low_ref, ...), custom_call_target="tpu_custom_call" | custom-call | tf_op jit(solution)/shard_map/pick/pallas_call | solution.py:145
  132.9 3.3 %all-to-all-start.1 = ((f32[32,1,2048]{2,1,0:T(1,128)}), f32[32,1,2048]{2,1,0:T(1,128)}, u32[]{:S(2)}, u32[]{:S(2)}) async-start(f32[32,1,2048]{2,1,0:T(1,128)} %get-tuple-element.5), calls=%async_computation.2 | async-start | bytes 524288 | tf_op jit(solution)/shard_map/all_to_all | solution.py:309
  136.4 0.7 mul.174
  137.0 0.7 mul.183
  137.7 1.9 reshape.213
  139.6 13.1 %gather_fusion = bf16[2048]{0:T(1024)(128)(2,1)S(1)} fusion(bf16[819200]{0:T(1024)(128)(2,1)S(1)} %reshape.213, s32[2048]{0:T(1024)S(1)} %broadcast_clamp_fusion), kind=kCustom, calls=%fused_computation | custom fusion | bytes 16384 | tf_op jit(solution)/shard_map/gather | solution.py:311
  152.7 0.6 convert_element_type.82
  153.3 6.5 %reduce-scatter.2.cloned.1.call-done = bf16[1,1280,640]{2,1,0:T(8,128)(2,1)} async-done(((bf16[4,1280,640]{2,1,0:T(8,128)(2,1)}), bf16[1,1280,640]{2,1,0:T(8,128)(2,1)}) %reduce-scatter.2.cloned.1.call-update) | async-done | bytes 1638416 | tf_op jit(solution)/shard_map/reduce_scatter | solution.py:294
  159.8 4.3 %all-to-all-start = ((bf16[8,160,640]{2,1,0:T(8,128)(2,1)}), bf16[8,160,640]{2,1,0:T(8,128)(2,1)}, u32[]{:S(2)}, u32[]{:S(2)}) async-start(bf16[8,160,640]{2,1,0:T(8,128)(2,1)} %bitcast.32), calls=%async_computation.1 | async-start | bytes 3276800 | tf_op jit(solution)/shard_map/all_to_all | solution.py:323
  164.1 15.2 %multiply_convert_fusion.1 = (bf16[1,8,80,1280]{3,2,0,1:T(8,128)(2,1)S(1)}, bf16[1,8,80,1280]{3,2,0,1:T(8,128)(2,1)S(1)}) fusion(s32[8,80]{1,0:T(8,128)S(1)} %mul.176, f32[8,80]{1,0:T(8,128)S(1)} %copy-done.7, f32[8,80]{1,0:T(8,128)S(1)} %copy-done.8), kind=kLoop, calls=%fused_computation.7 | loop fusion | flops 10649600 | bytes 3284480 | tf_op jit(solution)/shard_map/convert.2
  179.6 1.1 reduce_sum.11
  180.7 0.8 multiply_multiply_fusion
  181.5 42.2 %all_gather.7.val_ref = f32[32,1,2048]{2,1,0:T(1,128)S(1)} all-gather(f32[1,1,2048]{2,1,0:T(1,128)S(1)} %multiply_multiply_fusion), channel_id=1, replica_groups=mesh['band'=8,'lev'=4] {'lev','band'}, dimensions={0}, use_global_device_ids=true | all-gather | bytes 270336 | tf_op jit(solution)/shard_map/all_gather | solution.py:313
  223.7 36.1 %spread.1 = bf16[2,32,80,640]{3,2,1,0:T(8,128)(2,1)S(1)} custom-call(bf16[32,160,2048]{2,1,0:T(8,128)(2,1)} %get-tuple-element.4.g_ref, s32[32,1,2048]{2,1,0:T(1,128)S(1)} %get-tuple-element.11.row_ref, f32[32,1,2048]{2,1,0:T(1,128)S(1)} %all_gather.7.val_ref), custom_call_target="tpu_custom_call" | custom-call | tf_op jit(solution)/shard_map/spread/pallas_call | solution.py:201
  259.9 13.5 %analyse.1 = f32[64,80,160]{2,1,0:T(8,128)} custom-call(s32[80]{0:T(128)S(1)} %broadcast_subtract_fusion.thr_ref, bf16[64,80,640]{2,1,0:T(8,128)(2,1)S(1)} %bitcast.23, bf16[80,160,640]{2,1,0:T(8,128)(2,1)} %table_ref.3, f32[64,80,160]{2,1,0:T(8,128)S(1)} %bitcast.27, f32[1,160]{1,0:T(1,128)S(1)} %bitcast.28), custom_call_target="tpu_custom_call" | custom-call | tf_op jit(solution)/shard_map/analyse/pallas_call | solution.py:240
  273.4 5.5 %fusion.5 = bf16[640,1280]{1,0:T(8,128)(2,1)} fusion(bf16[640,1280]{1,0:T(8,128)(2,1)} %bitcast.30, bf16[1280,640]{1,0:T(8,128)(2,1)} %bitcast.3, bf16[1280,1280]{1,0:T(8,128)(2,1)S(1)} %bitcast.29), kind=kOutput, calls=%fused_computation.12 | convolution fusion | flops 2099609600 | bytes 8192000 | tf_op jit(solution)/shard_map/dot_general | solution.py:328
  (43 shorter events, 1.4 us)
Async XLA Ops:
  7.2 152.6 %reduce-scatter.2.cloned.1.call-start = ((), (), s32[]{:S(2)}) async-start(), calls=%async_computation.3 | async-start | bytes 8192000 | tf_op jit(solution)/shard_map/reduce_scatter | solution.py:294
  8.0 2.5 copy-start.2
  33.9 2.8 copy-start
  36.7 1.0 copy-start.5
  87.7 2.9 %copy-start.1 = (bf16[4,8,2,80,640]{4,3,2,1,0:T(8,128)(2,1)S(1)}, bf16[4,8,2,80,640]{4,3,2,1,0:T(8,128)(2,1)}, u32[]{:S(2)}) copy-start(bf16[4,8,2,80,640]{4,3,2,1,0:T(8,128)(2,1)} %copy-done) | copy-start | bytes 19660804
  90.6 45.7 %copy-start.6 = (s32[640]{0:T(1024)S(1)}, s32[640]{0:T(1024)}, u32[]{:S(2)}) copy-start(s32[640]{0:T(1024)} %param.10) | copy-start | bytes 7684
  90.6 47.1 %copy-start.4 = (bf16[8,80,1280]{2,1,0:T(8,128)(2,1)S(1)}, bf16[8,80,1280]{2,1,0:T(8,128)(2,1)}, u32[]{:S(2)}) copy-start(bf16[8,80,1280]{2,1,0:T(8,128)(2,1)} %param.11) | copy-start | bytes 4915204
  132.9 20.4 %all-to-all-start.1 = ((f32[32,1,2048]{2,1,0:T(1,128)}), f32[32,1,2048]{2,1,0:T(1,128)}, u32[]{:S(2)}, u32[]{:S(2)}) async-start(f32[32,1,2048]{2,1,0:T(1,128)} %get-tuple-element.5), calls=%async_computation.2 | async-start | bytes 524288 | tf_op jit(solution)/shard_map/all_to_all | solution.py:309
  139.6 24.5 %copy-start.7 = (f32[8,80]{1,0:T(8,128)S(1)}, f32[8,80]{1,0:T(8,128)}, u32[]{:S(2)}) copy-start(f32[8,80]{1,0:T(8,128)} %mul.174) | copy-start | bytes 7684
  139.6 24.5 %copy-start.8 = (f32[8,80]{1,0:T(8,128)S(1)}, f32[8,80]{1,0:T(8,128)}, u32[]{:S(2)}) copy-start(f32[8,80]{1,0:T(8,128)} %mul.183) | copy-start | bytes 7684
  159.8 113.6 %all-to-all-start = ((bf16[8,160,640]{2,1,0:T(8,128)(2,1)}), bf16[8,160,640]{2,1,0:T(8,128)(2,1)}, u32[]{:S(2)}, u32[]{:S(2)}) async-start(bf16[8,160,640]{2,1,0:T(8,128)(2,1)} %bitcast.32), calls=%async_computation.1 | async-start | bytes 3276800 | tf_op jit(solution)/shard_map/all_to_all | solution.py:323
  223.7 36.2 %slice-start = ((s8[5242880]{0:T(1024)(128)(4,1)}), s8[4194304]{0:T(1024)(128)(4,1)S(1)}, s32[]{:S(2)}) async-start(s8[5242880]{0:T(1024)(128)(4,1)} %bitcast.25), calls=%async_computation.4 | async-start | bytes 8388608
  223.7 36.2 %slice-start.1 = ((s8[5242880]{0:T(1024)(128)(4,1)}), s8[1048576]{0:T(1024)(128)(4,1)S(1)}, s32[]{:S(2)}) async-start(s8[5242880]{0:T(1024)(128)(4,1)} %bitcast.25), calls=%async_computation.5 | async-start | bytes 2097152
  223.7 36.2 %copy-start.3 = (f32[160]{0:T(256)S(1)}, f32[160]{0:T(256)}, u32[]{:S(2)}) copy-start(f32[160]{0:T(256)} %param.15) | copy-start | bytes 1924
Sparse Core Ops, SparseCore 0:
  36.8 122.9 reduce-scatter.1

commit v2 on v1

--- a/solution.py
+++ b/solution.py
@@ -9,7 +9,10 @@
 from jax.sharding import PartitionSpec as P
 
 S_CHUNK = 16
+SPREAD_CHUNK = 512
 O_CHUNK = 256
+VMEM_BYTES = 60 * 2**20
+HIGH_ROOM = 1024
 LOW = 32
 SPARSE_BYTES = 48 * 2**20
 
@@ -47,7 +50,7 @@
         ref[t, at, :] = piece
 
 
-def synth_kernel(thr_ref, spec_ref, table_ref, out_ref, spec_s, coef_s, row_s):
+def synth_kernel(thr_ref, spec_ref, table_ref, out_ref, spec_s, coef_s, *, first):
     parts, bands = out_ref.shape[0], out_ref.shape[1]
     cf, sc, deg = spec_ref.shape
     lats = table_ref.shape[2]
@@ -55,7 +58,7 @@
     l_own = lats // bands
     put_rows(spec_s, spec_ref[...].reshape(cf * sc, deg))
     degree = lax.broadcasted_iota(jnp.int32, (cf, deg), 1)
-    base = pl.program_id(0) * sc
+    base = (first + pl.program_id(0)) * sc
     for s in range(sc):
         a = get_rows(spec_s, pl.ds(s, cf, stride=sc), deg)
         a = jnp.where(degree >= thr_ref[base + s], a, 0.0).astype(jnp.bfloat16)
@@ -68,32 +71,33 @@
     def regroup(i, carry):
         k = i // 2
         c = i % 2
+        x = []
         for f in range(f_own):
             start = pl.multiple_of(((c * parts + k) * f_own + f) * sc, sc)
-            x = get_rows(coef_s, pl.ds(start, sc), lats)
-            for b in range(bands):
-                row_s[b, :, f * l_own : (f + 1) * l_own] = x[:, b * l_own : (b + 1) * l_own]
+            x.append(get_rows(coef_s, pl.ds(start, sc), lats).astype(jnp.bfloat16))
         for b in range(bands):
-            out_ref[k, b, c, :, :] = row_s[b].astype(jnp.bfloat16)
+            out_ref[k, b, c, :, :] = jnp.concatenate(
+                [x[f][:, b * l_own : (b + 1) * l_own] for f in range(f_own)], axis=1
+            )
         return carry
 
     lax.fori_loop(0, 2 * parts, regroup, 0)
 
 
-def synth(thr, spec, table, parts, bands):
-    cf, slots, deg = spec.shape
+def synth(thr, spec, table, parts, bands, first, count):
+    cf, _, deg = spec.shape
     lats = table.shape[2]
     f_own = cf // 2 // parts
     l_own = lats // bands
     sc = S_CHUNK
     return pl.pallas_call(
-        synth_kernel,
+        functools.partial(synth_kernel, first=first),
         grid_spec=pltpu.PrefetchScalarGridSpec(
             num_scalar_prefetch=1,
-            grid=(slots // sc,),
+            grid=(count,),
             in_specs=[
-                pl.BlockSpec((cf, sc, deg), lambda i, t: (0, i, 0)),
-                pl.BlockSpec((sc, deg, lats), lambda i, t: (i, 0, 0)),
+                pl.BlockSpec((cf, sc, deg), lambda i, t: (0, first + i, 0)),
+                pl.BlockSpec((sc, deg, lats), lambda i, t: (first + i, 0, 0)),
             ],
             out_specs=pl.BlockSpec(
                 (parts, bands, 2, sc, f_own * l_own), lambda i, t: (0, 0, 0, i, 0)
@@ -101,85 +105,94 @@
             scratch_shapes=[
                 pltpu.VMEM((-(-deg // 128), cf * sc, 128), jnp.float32),
                 pltpu.VMEM((-(-lats // 128), cf * sc, 128), jnp.float32),
-                pltpu.VMEM((bands, sc, f_own * l_own), jnp.float32),
             ],
         ),
-        out_shape=jax.ShapeDtypeStruct((parts, bands, 2, slots, f_own * l_own), jnp.bfloat16),
+        out_shape=jax.ShapeDtypeStruct((parts, bands, 2, count * sc, f_own * l_own), jnp.bfloat16),
         compiler_params=pltpu.CompilerParams(
-            dimension_semantics=("arbitrary",), vmem_limit_bytes=40 * 2**20
+            dimension_semantics=("arbitrary",), vmem_limit_bytes=VMEM_BYTES
         ),
         name="synth",
     )(thr, spec, table)
 
 
-def pick_kernel(coef_ref, row_ref, high_ref, low_ref, tab_ref, g_ref, p_ref):
-    cs, rows = coef_ref.shape[1], coef_ref.shape[2]
-    slots = cs // 2
-    obs = row_ref.shape[2]
-    highs = (tab_ref.shape[1] - 2 * LOW) // 2
-    row_id = lax.broadcasted_iota(jnp.int32, (rows, O_CHUNK), 0)
-    high_id = lax.broadcasted_iota(jnp.int32, (highs, O_CHUNK), 0)
-    low_id = lax.broadcasted_iota(jnp.int32, (LOW, O_CHUNK), 0)
+def one_hot(cells, rows, values=None):
+    row = (cells // (LOW * HIGH_ROOM)).astype(jnp.int16)
+    row_id = lax.broadcasted_iota(jnp.int16, (rows, cells.shape[1]), 0)
+    values = jnp.ones(cells.shape, jnp.bfloat16) if values is None else values.astype(jnp.bfloat16)
+    return jnp.where(row_id == row, values, jnp.zeros_like(values))
+
+
+def pick_kernel(cell_ref, tab_ref, *refs):
+    coef_refs, (g_ref, p_ref) = refs[:-2], refs[-2:]
+    coef = jnp.concatenate([r[0] for r in coef_refs], axis=0)
+    rows = coef.shape[1]
+    slots = coef.shape[0] // 2
+    obs = cell_ref.shape[2]
     for o in range(obs // O_CHUNK):
         at = slice(o * O_CHUNK, (o + 1) * O_CHUNK)
-        a = (high_id == high_ref[0, :, at]).astype(jnp.float32)
-        b = (low_id == low_ref[0, :, at]).astype(jnp.float32)
-        hot = jnp.concatenate([a, a, b, b], axis=0).astype(jnp.bfloat16)
-        parts = jnp.dot(tab_ref[...], hot, preferred_element_type=jnp.float32)
-        uc, us = parts[:slots], parts[slots : 2 * slots]
-        vc, vs = parts[2 * slots : 3 * slots], parts[3 * slots :]
-        gc = (uc * vc - us * vs).astype(jnp.bfloat16)
-        gs = (-(us * vc + uc * vs)).astype(jnp.bfloat16)
-        g_ref[0, :slots, at] = gc
-        g_ref[0, slots:, at] = gs
-        pick = (row_id == row_ref[0, :, at]).astype(jnp.float32).astype(jnp.bfloat16)
-        t = jnp.dot(coef_ref[0], pick, preferred_element_type=jnp.float32)
-        p = t[:slots] * gc.astype(jnp.float32) + t[slots:] * gs.astype(jnp.float32)
-        p_ref[0, :, at] = jnp.sum(p, axis=0, keepdims=True)
-
-
-def pick(coef, row, high, low, tab):
-    blocks, cs, rows = coef.shape
-    obs = row.shape[2]
+        t = jnp.dot(coef, one_hot(cell_ref[0, :, at], rows), preferred_element_type=jnp.float32)
+        for lane in range(0, O_CHUNK, 128):
+            own_at = slice(o * O_CHUNK + lane, o * O_CHUNK + lane + 128)
+            cell = cell_ref[0, :, own_at]
+            high = jnp.broadcast_to((cell // LOW) & (HIGH_ROOM - 1), (slots, 128))
+            low = jnp.broadcast_to(cell & (LOW - 1), (slots, 128))
+
+            def look_up(i, index):
+                return jnp.take_along_axis(tab_ref[i], index, axis=1, mode="promise_in_bounds")
+
+            uc, us = look_up(0, high), look_up(1, high)
+            vc, vs = look_up(2, low), look_up(3, low)
+            gc = (uc * vc - us * vs).astype(jnp.bfloat16)
+            gs = (-(us * vc + uc * vs)).astype(jnp.bfloat16)
+            g_ref[0, :slots, own_at] = gc
+            g_ref[0, slots:, own_at] = gs
+            order, first = [], 0
+            for r in coef_refs:
+                own = slice(first, first + r.shape[1] // 2)
+                order += [gc[own], gs[own]]
+                first = own.stop
+            p = t[:, lane : lane + 128] * jnp.concatenate(order, axis=0).astype(jnp.float32)
+            p_ref[0, :, own_at] = jnp.sum(p, axis=0, keepdims=True)
+
+
+def pick(coefs, cells, tab):
+    blocks, _, rows = coefs[0].shape
+    cs = sum(x.shape[1] for x in coefs)
+    obs = cells.shape[2]
     one = pl.BlockSpec((1, 1, obs), lambda i: (i, 0, 0))
     return pl.pallas_call(
         pick_kernel,
         grid=(blocks,),
-        in_specs=[
-            pl.BlockSpec((1, cs, rows), lambda i: (i, 0, 0)),
-            one,
-            one,
-            one,
-            pl.BlockSpec(tab.shape, lambda i: (0, 0)),
-        ],
+        in_specs=[one, pl.BlockSpec(tab.shape, lambda i: (0, 0, 0))]
+        + [pl.BlockSpec((1, x.shape[1], rows), lambda i: (i, 0, 0)) for x in coefs],
         out_specs=[pl.BlockSpec((1, cs, obs), lambda i: (i, 0, 0)), one],
         out_shape=[
             jax.ShapeDtypeStruct((blocks, cs, obs), jnp.bfloat16),
             jax.ShapeDtypeStruct((blocks, 1, obs), jnp.float32),
         ],
         compiler_params=pltpu.CompilerParams(
-            dimension_semantics=("arbitrary",), vmem_limit_bytes=40 * 2**20
+            dimension_semantics=("arbitrary",), vmem_limit_bytes=VMEM_BYTES
         ),
         name="pick",
-    )(coef, row, high, low, tab)
-
-
-def spread_kernel(g_ref, row_ref, val_ref, out_ref, hot_s, coef_s, *, bands):
+    )(cells, tab, *coefs)
+
+
+def spread_kernel(g_ref, cell_ref, val_ref, out_ref, coef_s, *, bands):
     cs, obs = g_ref.shape[1], g_ref.shape[2]
     slots = cs // 2
     f_own = out_ref.shape[1]
     lats = out_ref.shape[3]
     l_own = lats // bands
     rows = f_own * l_own
-    row_id = lax.broadcasted_iota(jnp.int32, (rows, O_CHUNK), 0)
-    for o in range(obs // O_CHUNK):
-        at = slice(o * O_CHUNK, (o + 1) * O_CHUNK)
-        hot_s[:, at] = jnp.where(row_id == row_ref[0, :, at], val_ref[0, :, at], 0.0).astype(
-            jnp.bfloat16
-        )
-    acc = lax.dot_general(
-        hot_s[...], g_ref[0], (((1,), (1,)), ((), ())), preferred_element_type=jnp.float32
-    )
+    acc = 0.0
+    for o in range(obs // SPREAD_CHUNK):
+        at = slice(o * SPREAD_CHUNK, (o + 1) * SPREAD_CHUNK)
+        acc = acc + lax.dot_general(
+            one_hot(cell_ref[0, :, at], rows, val_ref[0, :, at]),
+            g_ref[0, :, at],
+            (((1,), (1,)), ((), ())),
+            preferred_element_type=jnp.float32,
+        )
     b = pl.program_id(1)
     start = pl.multiple_of(b * l_own, 8)
     for f in range(f_own):
@@ -193,10 +206,9 @@
             out_ref[1, f] = t[slots:]
 
 
-def spread(g, row, val, parts, bands, fields, lats):
-    blocks, cs, obs = g.shape
+def spread(g, cells, val, parts, bands, fields, lats):
+    _, cs, obs = g.shape
     f_own = fields // parts
-    l_own = lats // bands
     one = pl.BlockSpec((1, 1, obs), lambda k, b: (k * bands + b, 0, 0))
     return pl.pallas_call(
         functools.partial(spread_kernel, bands=bands),
@@ -205,14 +217,50 @@
         out_specs=pl.BlockSpec((2, f_own, cs // 2, lats), lambda k, b: (0, k, 0, 0)),
         out_shape=jax.ShapeDtypeStruct((2, fields, cs // 2, lats), jnp.bfloat16),
         scratch_shapes=[
-            pltpu.VMEM((f_own * l_own, obs), jnp.bfloat16),
             pltpu.VMEM((f_own, lats, cs), jnp.float32),
         ],
         compiler_params=pltpu.CompilerParams(
-            dimension_semantics=("arbitrary", "arbitrary"), vmem_limit_bytes=40 * 2**20
+            dimension_semantics=("arbitrary", "arbitrary"), vmem_limit_bytes=VMEM_BYTES
         ),
         name="spread",
-    )(g, row, val)
+    )(g, cells, val)
+
+
+def fourier_kernel(base_ref, step_ref, out_ref):
+    bc, bs = base_ref[0], base_ref[1]
+    for t in range(out_ref.shape[3] // 128):
+        at = slice(t * 128, (t + 1) * 128)
+        sc, ss = step_ref[0, :, t : t + 1], step_ref[1, :, t : t + 1]
+        out_ref[0, 0, :, at] = (sc * bc - ss * bs).astype(jnp.bfloat16)
+        out_ref[0, 1, :, at] = (-(ss * bc + sc * bs)).astype(jnp.bfloat16)
+
+
+def fourier_rows(wave_order, width, slots):
+    count = wave_order.shape[0]
+    factor = jnp.where(wave_order == 0, 1.0, 2.0).astype(jnp.float32)[:, None]
+
+    def pair(columns, scale):
+        phase = wave_order[:, None] * columns[None, :] % width
+        angle = phase.astype(jnp.float32) * (2.0 * math.pi / width)
+        return jnp.stack([scale * jnp.cos(angle), scale * jnp.sin(angle)])
+
+    base = pair(jnp.arange(128, dtype=jnp.int32), 1.0)
+    step = pair(128 * jnp.arange(width // 128, dtype=jnp.int32), factor)
+    rows = pl.pallas_call(
+        fourier_kernel,
+        grid=(count // slots,),
+        in_specs=[
+            pl.BlockSpec((2, slots, 128), lambda i: (0, i, 0)),
+            pl.BlockSpec((2, slots, width // 128), lambda i: (0, i, 0)),
+        ],
+        out_specs=pl.BlockSpec((1, 2, slots, width), lambda i: (i, 0, 0, 0)),
+        out_shape=jax.ShapeDtypeStruct((count // slots, 2, slots, width), jnp.bfloat16),
+        compiler_params=pltpu.CompilerParams(
+            dimension_semantics=("arbitrary",), vmem_limit_bytes=VMEM_BYTES
+        ),
+        name="fourier",
+    )(base, step)
+    return rows
 
 
 def analyse_kernel(thr_ref, coef_ref, table_ref, spec_ref, inv_ref, out_ref, coef_s, out_s):
@@ -256,29 +304,26 @@
         ),
         out_shape=jax.ShapeDtypeStruct((cf, slots, deg), jnp.float32),
         compiler_params=pltpu.CompilerParams(
-            dimension_semantics=("arbitrary",), vmem_limit_bytes=40 * 2**20
+            dimension_semantics=("arbitrary",), vmem_limit_bytes=VMEM_BYTES
         ),
         name="analyse",
     )(thr, coef, table, spec, inv_var)
 
 
 def observation_table(waves, width):
-    highs = width // LOW
     factor = jnp.where(waves == 0, 1.0, 2.0).astype(jnp.float32)[:, None]
-
-    def pair(columns, scale):
-        phase = waves[:, None] * columns[None, :] % width
-        angle = phase.astype(jnp.float32) * (2.0 * math.pi / width)
-        exact = jnp.concatenate([scale * jnp.cos(angle), scale * jnp.sin(angle)], axis=0)
-        near = exact.astype(jnp.bfloat16)
-        rest = (exact - near.astype(jnp.float32)).astype(jnp.bfloat16)
-        return jnp.concatenate([near, rest], axis=1)
-
-    u = pair(LOW * jnp.arange(highs, dtype=jnp.int32), factor)
-    v = pair(jnp.arange(LOW, dtype=jnp.int32), 1.0)
-    top = jnp.concatenate([u, jnp.zeros((u.shape[0], v.shape[1]), u.dtype)], axis=1)
-    bottom = jnp.concatenate([jnp.zeros((v.shape[0], u.shape[1]), u.dtype), v], axis=1)
-    return jnp.concatenate([top, bottom], axis=0)
+    columns = jnp.arange(128, dtype=jnp.int32)
+
+    def pair(step, scale):
+        angle = (waves[:, None] * (step * columns)[None, :] % width).astype(jnp.float32)
+        angle = angle * (2.0 * math.pi / width)
+        return [scale * jnp.cos(angle), scale * jnp.sin(angle)]
+
+    return jnp.stack(pair(LOW, factor) + pair(1, 1.0))
+
+
+def chunk_counts(steps):
+    return [steps] if steps < 2 else [steps - steps * 2 // 5, steps * 2 // 5]
 
 
 def sparse_shards(parts, bands, spectral, legendre, wave_order, jacobian, obs_cell, innovation, obs_weight, inv_var):
@@ -290,28 +335,35 @@
     thr = own_waves - lax.axis_index("lev") * degrees
     spec = spectral.reshape(2 * fields, slots, degrees)
 
-    partial = synth(thr, spec, legendre, parts, bands)
-    summed = lax.psum_scatter(
-        partial.reshape(parts, bands * 2 * slots, f_own * l_own), "lev", scatter_dimension=0, tiled=True
-    )
-
-    cells = obs_cell.reshape(1, 1, obs)
-    all_cells = lax.all_gather(cells, ("lev", "band"), axis=0, tiled=True)
-    row = all_cells // width
-    lon = all_cells % width
+    def to_all(x):
+        copies = jnp.broadcast_to(x.reshape(1, 1, obs), (parts * bands, 1, obs))
+        return lax.all_to_all(copies, ("lev", "band"), split_axis=0, concat_axis=0, tiled=True)
+
+    lon = obs_cell % width
+    cells = to_all((obs_cell // width) * (HIGH_ROOM * LOW) + lon)
+    counts = chunk_counts(slots // S_CHUNK)
+    partial, summed, first = [], [], 0
+    for count in counts:
+        x = synth(thr, spec, legendre, parts, bands, first, count)
+        first += count
+        x = x.reshape(parts, bands * 2 * count * S_CHUNK, f_own * l_own)
+        partial.append(x)
+        summed.append(lax.psum_scatter(x, "lev", scatter_dimension=0, tiled=True))
+
     g, p = pick(
-        partial.reshape(parts * bands, 2 * slots, f_own * l_own),
-        row,
-        lon // LOW,
-        lon % LOW,
+        [x.reshape(parts * bands, -1, f_own * l_own) for x in partial],
+        cells,
         observation_table(own_waves, width),
     )
     at_owner = lax.all_to_all(p, ("lev", "band"), split_axis=0, concat_axis=0, tiled=True)
+    jac_at = jacobian.reshape(-1)[obs_cell.reshape(-1)].astype(jnp.float32)
     grid_at = jnp.sum(at_owner.reshape(parts * bands, obs), axis=0)
-    jac_at = jacobian.reshape(-1)[obs_cell.reshape(-1)].astype(jnp.float32)
     misfit = obs_weight.reshape(-1) * (grid_at * jac_at - innovation.reshape(-1))
-    val = lax.all_gather((misfit * jac_at).reshape(1, 1, obs), ("lev", "band"), axis=0, tiled=True)
-    coef_adj = spread(g, row, val, parts, bands, fields, lats)
+    val = to_all(misfit * jac_at)
+    fourier = fourier_rows(wave_order, width, slots)
+    val, early, fourier = lax.optimization_barrier((val, summed[:-1], fourier))
+    coef_adj = spread(g, cells, val, parts, bands, fields, lats)
+    coef_adj, late = lax.optimization_barrier((coef_adj, summed[-1]))
     gradient = analyse(
         thr,
         coef_adj.reshape(2 * fields, slots, lats),
@@ -320,17 +372,19 @@
         inv_var.reshape(1, degrees),
     ).reshape(spectral.shape)
 
-    by_latitude = lax.all_to_all(
-        summed.reshape(bands, 2 * slots, f_own * l_own), "band", split_axis=0, concat_axis=0, tiled=True
-    )
-    fourier = fourier_table(wave_order, width).reshape(2, bands, slots, width)
-    fourier = fourier.transpose(1, 0, 2, 3).reshape(bands * 2 * slots, width)
-    grid = lax.dot_general(
-        by_latitude.reshape(bands * 2 * slots, f_own * l_own),
-        fourier,
-        (((0,), (0,)), ((), ())),
-        preferred_element_type=jnp.float32,
-    )
+    grid, first = 0.0, 0
+    for count, x in zip(counts, [*early, late]):
+        n = count * S_CHUNK
+        x = lax.all_to_all(
+            x.reshape(bands, 2 * n, f_own * l_own), "band", split_axis=0, concat_axis=0, tiled=True
+        )
+        grid = grid + lax.dot_general(
+            x.reshape(bands, 2, n, f_own * l_own),
+            fourier[:, :, first : first + n],
+            (((0, 1, 2), (0, 1, 2)), ((), ())),
+            preferred_element_type=jnp.float32,
+        )
+        first += n
     model_grid = (grid * jacobian.reshape(f_own * l_own, width)).astype(jnp.bfloat16)
     return model_grid.reshape(jacobian.shape), gradient
 
@@ -393,7 +447,10 @@
             and slots % S_CHUNK == 0
             and l_own % 16 == 0
             and obs % O_CHUNK == 0
+            and obs % SPREAD_CHUNK == 0
+            and width // LOW <= 128
             and width % LOW == 0
+            and width % 128 == 0
         )
         args = (spectral, legendre, wave_order, jacobian, obs_cell, innovation, obs_weight, inv_var)
         return sparse_shards(parts, bands, *args) if fits else dense_shards(*args)

time: 287 us -> 224 us (0.78)
  blocking collectives: 88.5 us -> 0 us
  waiting for transfers between devices: 6.5 us -> 26.9 us
  other arithmetic: 23.1 us -> 5.97 us
  starting transfers between devices: 7.66 us -> 24.6 us
  Pallas kernels: 115 us -> 122 us
  local copies, waits for them, and re-layouts: 24.7 us -> 18.5 us
  matrix products: 5.45 us -> 9.19 us
    all_gather x2 -> x0, blocking collectives: 88.5 us -> none  [the longest x1 46.3 us: sparse_shards(): all_cells = lax.all_gather(cells, ('lev', 'band'), axis=0, tiled=True)]
    all_to_all x1 -> x4, waiting for transfers between devices: 0.01 us -> 26.8 us  [the longest x2 20.1 us: to_all(): lax.all_to_all(copies, ('lev', 'band'), split_axis=0, concat_axis=0, tile...]
    all_to_all x1 -> x4, starting transfers between devices: 4.31 us -> 21.8 us  [the longest x2 13.2 us: to_all(): lax.all_to_all(copies, ('lev', 'band'), split_axis=0, concat_axis=0, tile...]
    another operation x2 -> x3, other arithmetic: 15.5 us -> 1.61 us  [the longest x2 0.93 us: pair(): return jnp.stack([scale * jnp.cos(angle), scale * jnp.sin(angle)])]
    unnamed x22 -> x16, local copies, waits for them, and re-layouts: 8.13 us -> 0.72 us
    reduce_scatter x1 -> x2, waiting for transfers between devices: 6.47 us -> 0.01 us  [sparse_shards(): summed.append(lax.psum_scatter(x, 'lev', scatter_dimension=0, tiled=True))]
    dot_general x1 -> x2, matrix products: 5.45 us -> 9.19 us  [sparse_shards(): lax.dot_general(x.reshape(bands, 2, n, f_own * l_own), fourier[:, :, firs...]
    select_n x3 -> x1, other arithmetic: 3.71 us -> 0.01 us  [fourier_rows(): factor = jnp.where(wave_order == 0, 1.0, 2.0).astype(jnp.float32)[:, None]]
  transfers between devices with their start and end apart: 3 -> 7, of which waited for: 1 -> 3; matrix products, arithmetic and copies ran while one was open for 14% -> 12% of each run, Pallas kernels for 32% -> 49%
where the time goes in v2:
time: 224 us; the launch traced here: 221 us
  Pallas kernels  122 us (54%)
  waiting for transfers between devices  26.9 us (12%)
  starting transfers between devices  24.6 us (11%)
  local copies, waits for them, and re-layouts  18.5 us (8%)
  between operations  14.3 us (6%)
  matrix products  9.19 us (4%)
  other arithmetic  5.97 us (3%)
    pallas_call x1, Pallas kernels, spread(): pl.pallas_call(functools.partial(spread_kernel, bands=bands), grid=(parts...  38.6 us
    pallas_call x1, Pallas kernels, pick(): pl.pallas_call(pick_kernel, grid=(blocks,), in_specs=[one, pl.BlockSpec(t...  36.5 us
    pallas_call x2, Pallas kernels, synth(): pl.pallas_call(functools.partial(synth_kernel, first=first), grid_spec=pl...  23.3 us
    all_to_all x2, waiting for transfers between devices, to_all(): lax.all_to_all(copies, ('lev', 'band'), split_axis=0, concat_axis=0, tile...  20.1 us
    pallas_call x1, Pallas kernels, analyse(): pl.pallas_call(analyse_kernel, grid_spec=pltpu.PrefetchScalarGridSpec(num...  16.6 us
    all_to_all x2, starting transfers between devices, to_all(): lax.all_to_all(copies, ('lev', 'band'), split_axis=0, concat_axis=0, tile...  13.2 us
    gather x1, local copies, waits for them, and re-layouts, sparse_shards(): jac_at = jacobian.reshape(-1)[obs_cell.reshape(-1)].astype(jnp.float32)  13.1 us
    dot_general x2, matrix products, sparse_shards(): lax.dot_general(x.reshape(bands, 2, n, f_own * l_own), fourier[:, :, firs...  9.19 us
  transfers between devices with their start and end apart: 7, of which 3 were waited for; matrix products, arithmetic and copies ran while one was open for 12% of the time, Pallas kernels for 49%

profile of v2, /device:TPU:0, one launch (start us, length us, event | category | flops | bytes accessed | tf_op | source)
XLA Modules:
  0.0 221.3 jit_solution(7238153625046106967)
XLA Ops:
  7.2 1.4 broadcast_subtract_fusion
  8.6 13.2 %synth.2 = bf16[4,8,2,48,640]{4,3,2,1,0:T(8,128)(2,1)} custom-call(s32[80]{0:T(128)} %get-tuple-element.16.thr_ref, f32[64,80,160]{2,1,0:T(8,128)} %bitcast.38, bf16[80,160,640]{2,1,0:T(8,128)(2,1)} %table_ref.5), custom_call_target="tpu_custom_call" | custom-call | tf_op jit(solution)/shard_map/synth/pallas_call | solution.py:93
  21.8 10.1 %synth.3 = bf16[4,8,2,32,640]{4,3,2,1,0:T(8,128)(2,1)} custom-call(s32[80]{0:T(128)} %get-tuple-element.16.thr_ref, f32[64,80,160]{2,1,0:T(8,128)} %bitcast.39, bf16[80,160,640]{2,1,0:T(8,128)(2,1)} %table_ref.5), custom_call_target="tpu_custom_call" | custom-call | tf_op jit(solution)/shard_map/synth/pallas_call | solution.py:93
  32.1 0.8 broadcast_in_dim.42
  32.9 7.3 %all-to-all-start = ((s32[32,1,2048]{2,1,0:T(1,128)}), s32[32,1,2048]{2,1,0:T(1,128)S(1)}, u32[]{:S(2)}, u32[]{:S(2)}) async-start(s32[32,1,2048]{2,1,0:T(1,128)} %broadcast_in_dim.42), calls=%async_computation | async-start | bytes 524288 | tf_op jit(solution)/shard_map/all_to_all | solution.py:340
  40.3 1.9 reshape.560
  43.3 14.8 %all-to-all-done.cell_ref = s32[32,1,2048]{2,1,0:T(1,128)S(1)} async-done(((s32[32,1,2048]{2,1,0:T(1,128)}), s32[32,1,2048]{2,1,0:T(1,128)S(1)}, u32[]{:S(2)}, u32[]{:S(2)}) %all-to-all-start) | async-done | bytes 262176 | tf_op jit(solution)/shard_map/all_to_all | solution.py:340
  58.8 36.5 %pick.1 = (bf16[32,160,2048]{2,1,0:T(8,128)(2,1)}, f32[32,1,2048]{2,1,0:T(1,128)}) custom-call(s32[32,1,2048]{2,1,0:T(1,128)} %copy-done.1, f32[4,80,128]{2,1,0:T(8,128)} %pad_maximum_fusion.1.tab_ref, bf16[32,96,640]{2,1,0:T(8,128)(2,1)} %bitcast.42, bf16[32,64,640]{2,1,0:T(8,128)(2,1)} %bitcast.45), custom_call_target="tpu_custom_call" | custom-call | tf_op jit(solution)/shard_map/pick/pallas_call | solution.py:163
  95.3 2.8 %all-to-all-start.1 = ((f32[32,1,2048]{2,1,0:T(1,128)}), f32[32,1,2048]{2,1,0:T(1,128)S(1)}, u32[]{:S(2)}, u32[]{:S(2)}) async-start(f32[32,1,2048]{2,1,0:T(1,128)} %get-tuple-element.9), calls=%async_computation.1 | async-start | bytes 524288 | tf_op jit(solution)/shard_map/all_to_all | solution.py:358
  98.1 13.1 %gather_fusion = bf16[2048]{0:T(1024)(128)(2,1)S(1)} fusion(bf16[819200]{0:T(1024)(128)(2,1)S(1)} %reshape.560, s32[2048]{0:T(1024)S(1)} %broadcast_clamp_fusion), kind=kCustom, calls=%fused_computation | custom fusion | bytes 16384 | tf_op jit(solution)/shard_map/gather | solution.py:359
  112.3 5.8 %all-to-all-start.2 = ((f32[32,1,2048]{2,1,0:T(1,128)}), f32[32,1,2048]{2,1,0:T(1,128)S(1)}, u32[]{:S(2)}, u32[]{:S(2)}) async-start(f32[32,1,2048]{2,1,0:T(1,128)} %broadcast_in_dim.46), calls=%async_computation.2 | async-start | bytes 524288 | tf_op jit(solution)/shard_map/all_to_all | solution.py:340
  118.2 0.9 cosine_multiply_fusion.1
  119.1 1.1 copy.10.step_ref
  120.3 1.4 fusion.10
  121.7 0.9 pad_maximum_fusion.base_ref
  122.5 6.8 %fourier.1 = bf16[8,2,80,1280]{3,2,1,0:T(8,128)(2,1)} custom-call(f32[2,640,128]{2,1,0:T(8,128)} %pad_maximum_fusion.base_ref, f32[2,640,10]{2,1,0:T(8,128)} %copy.10.step_ref), custom_call_target="tpu_custom_call" | custom-call | tf_op jit(solution)/shard_map/fourier/pallas_call | solution.py:249
  129.3 5.2 %all-to-all-done.2.val_ref = f32[32,1,2048]{2,1,0:T(1,128)S(1)} async-done(((f32[32,1,2048]{2,1,0:T(1,128)}), f32[32,1,2048]{2,1,0:T(1,128)S(1)}, u32[]{:S(2)}, u32[]{:S(2)}) %all-to-all-start.2) | async-done | bytes 262176 | tf_op jit(solution)/shard_map/all_to_all | solution.py:340
  134.6 4.4 %all-to-all-start.3 = ((bf16[8,96,640]{2,1,0:T(8,128)(2,1)}), bf16[8,96,640]{2,1,0:T(8,128)(2,1)}, u32[]{:S(2)}, u32[]{:S(2)}) async-start(bf16[8,96,640]{2,1,0:T(8,128)(2,1)} %bitcast.48), calls=%async_computation.4 | async-start | bytes 1966080 | tf_op jit(solution)/shard_map/all_to_all | solution.py:378
  139.0 38.6 %spread.1 = bf16[2,32,80,640]{3,2,1,0:T(8,128)(2,1)} custom-call(bf16[32,160,2048]{2,1,0:T(8,128)(2,1)} %get-tuple-element.12.g_ref, s32[32,1,2048]{2,1,0:T(1,128)} %copy-done.1, f32[32,1,2048]{2,1,0:T(1,128)} %copy-done.3), custom_call_target="tpu_custom_call" | custom-call | tf_op jit(solution)/shard_map/spread/pallas_call | solution.py:213
  177.6 16.6 %analyse.1 = f32[64,80,160]{2,1,0:T(8,128)} custom-call(s32[80]{0:T(128)} %get-tuple-element.16.thr_ref, bf16[64,80,640]{2,1,0:T(8,128)(2,1)} %bitcast.43, bf16[80,160,640]{2,1,0:T(8,128)(2,1)} %table_ref.5, f32[64,80,160]{2,1,0:T(8,128)} %bitcast.40, f32[1,160]{1,0:T(1,128)} %bitcast.55), custom_call_target="tpu_custom_call" | custom-call | tf_op jit(solution)/shard_map/analyse/pallas_call | solution.py:288
  194.3 4.2 %all-to-all-start.4 = ((bf16[8,64,640]{2,1,0:T(8,128)(2,1)}), bf16[8,64,640]{2,1,0:T(8,128)(2,1)}, u32[]{:S(2)}, u32[]{:S(2)}) async-start(bf16[8,64,640]{2,1,0:T(8,128)(2,1)} %bitcast.49), calls=%async_computation.6 | async-start | bytes 1310720 | tf_op jit(solution)/shard_map/all_to_all | solution.py:378
  198.5 4.3 %convolution_bitcast_fusion.1 = f32[640,1280]{1,0:T(8,128)} fusion(bf16[8,2,48,640]{3,2,1,0:T(8,128)(2,1)} %bitcast.11, bf16[8,2,80,1280]{3,2,1,0:T(8,128)(2,1)S(1)} %copy-done), kind=kOutput, calls=%fused_computation.4 | convolution fusion | flops 1258291200 | bytes 6225920 | tf_op jit(solution)/shard_map/dot_general | solution.py:381
  202.8 6.8 %all-to-all-done.4 = bf16[8,64,640]{2,1,0:T(8,128)(2,1)} async-done(((bf16[8,64,640]{2,1,0:T(8,128)(2,1)}), bf16[8,64,640]{2,1,0:T(8,128)(2,1)}, u32[]{:S(2)}, u32[]{:S(2)}) %all-to-all-start.4) | async-done | bytes 655392 | tf_op jit(solution)/shard_map/all_to_all | solution.py:378
  209.6 4.8 %fusion.2 = bf16[640,1280]{1,0:T(8,128)(2,1)} fusion(bf16[640,1280]{1,0:T(8,128)(2,1)} %bitcast.47, f32[640,1280]{1,0:T(8,128)} %convolution_bitcast_fusion.1, bf16[8,2,32,640]{3,2,1,0:T(8,128)(2,1)} %bitcast.16, bf16[8,2,80,1280]{3,2,1,0:T(8,128)(2,1)S(1)} %copy-done), kind=kOutput, calls=%fused_computation.5 | convolution fusion | flops 842137600 | bytes 8519680 | tf_op jit(solution)/shard_map/dot_general | solution.py:381
  (38 shorter events, 3.1 us)
Async XLA Ops:
  7.2 127.4 %reduce-scatter.3.cloned.1.call-start = ((), (), s32[]{:S(2)}) async-start(), calls=%async_computation.7 | async-start | bytes 4915200 | tf_op jit(solution)/shard_map/reduce_scatter | solution.py:351
  21.8 10.2 %copy-start.5 = (s32[1,1,2048]{2,1,0:T(1,128)S(1)}, s32[1,1,2048]{2,1,0:T(1,128)}, u32[]{:S(2)}) copy-start(s32[1,1,2048]{2,1,0:T(1,128)} %param.12) | copy-start | bytes 24580
  21.8 155.8 %reduce-scatter.5.cloned.1.call-start = ((), (), s32[]{:S(2)}) async-start(), calls=%async_computation.8 | async-start | bytes 3276800 | tf_op jit(solution)/shard_map/reduce_scatter | solution.py:351
  32.0 8.3 %copy-start.2 = (bf16[8,80,1280]{2,1,0:T(8,128)(2,1)S(1)}, bf16[8,80,1280]{2,1,0:T(8,128)(2,1)}, u32[]{:S(2)}) copy-start(bf16[8,80,1280]{2,1,0:T(8,128)(2,1)} %param.11) | copy-start | bytes 4915204
  32.9 25.2 %all-to-all-start = ((s32[32,1,2048]{2,1,0:T(1,128)}), s32[32,1,2048]{2,1,0:T(1,128)S(1)}, u32[]{:S(2)}, u32[]{:S(2)}) async-start(s32[32,1,2048]{2,1,0:T(1,128)} %broadcast_in_dim.42), calls=%async_computation | async-start | bytes 524288 | tf_op jit(solution)/shard_map/all_to_all | solution.py:340
  58.1 0.7 copy-start.1
  95.3 15.9 %copy-start.4 = (s32[640]{0:T(1024)S(1)}, s32[640]{0:T(1024)}, u32[]{:S(2)}) copy-start(s32[640]{0:T(1024)} %param.10) | copy-start | bytes 7684
  95.3 16.1 %copy-start.6 = (f32[1,1,2048]{2,1,0:T(1,128)S(1)}, f32[1,1,2048]{2,1,0:T(1,128)}, u32[]{:S(2)}) copy-start(f32[1,1,2048]{2,1,0:T(1,128)} %param.14) | copy-start | bytes 24580
  95.3 16.1 %copy-start.7 = (f32[1,1,2048]{2,1,0:T(1,128)S(1)}, f32[1,1,2048]{2,1,0:T(1,128)}, u32[]{:S(2)}) copy-start(f32[1,1,2048]{2,1,0:T(1,128)} %param.13) | copy-start | bytes 24580
  95.3 15.9 %all-to-all-start.1 = ((f32[32,1,2048]{2,1,0:T(1,128)}), f32[32,1,2048]{2,1,0:T(1,128)S(1)}, u32[]{:S(2)}, u32[]{:S(2)}) async-start(f32[32,1,2048]{2,1,0:T(1,128)} %get-tuple-element.9), calls=%async_computation.1 | async-start | bytes 524288 | tf_op jit(solution)/shard_map/all_to_all | solution.py:358
  112.3 22.2 %all-to-all-start.2 = ((f32[32,1,2048]{2,1,0:T(1,128)}), f32[32,1,2048]{2,1,0:T(1,128)S(1)}, u32[]{:S(2)}, u32[]{:S(2)}) async-start(f32[32,1,2048]{2,1,0:T(1,128)} %broadcast_in_dim.46), calls=%async_computation.2 | async-start | bytes 524288 | tf_op jit(solution)/shard_map/all_to_all | solution.py:340
  134.5 4.4 %copy-start.3 = (f32[32,1,2048]{2,1,0:T(1,128)}, f32[32,1,2048]{2,1,0:T(1,128)S(1)}, u32[]{:S(2)}) copy-start(f32[32,1,2048]{2,1,0:T(1,128)S(1)} %all-to-all-done.2.val_ref) | copy-start | bytes 786436
  134.6 59.7 %all-to-all-start.3 = ((bf16[8,96,640]{2,1,0:T(8,128)(2,1)}), bf16[8,96,640]{2,1,0:T(8,128)(2,1)}, u32[]{:S(2)}, u32[]{:S(2)}) async-start(bf16[8,96,640]{2,1,0:T(8,128)(2,1)} %bitcast.48), calls=%async_computation.4 | async-start | bytes 1966080 | tf_op jit(solution)/shard_map/all_to_all | solution.py:378
  177.6 20.9 %copy-start = (bf16[8,2,80,1280]{3,2,1,0:T(8,128)(2,1)S(1)}, bf16[8,2,80,1280]{3,2,1,0:T(8,128)(2,1)}, u32[]{:S(2)}) copy-start(bf16[8,2,80,1280]{3,2,1,0:T(8,128)(2,1)} %fourier.1) | copy-start | bytes 9830404
  194.3 15.3 %all-to-all-start.4 = ((bf16[8,64,640]{2,1,0:T(8,128)(2,1)}), bf16[8,64,640]{2,1,0:T(8,128)(2,1)}, u32[]{:S(2)}, u32[]{:S(2)}) async-start(bf16[8,64,640]{2,1,0:T(8,128)(2,1)} %bitcast.49), calls=%async_computation.6 | async-start | bytes 1310720 | tf_op jit(solution)/shard_map/all_to_all | solution.py:378
Sparse Core Ops, SparseCore 0:
  21.9 79.4 reduce-scatter.2
  103.7 59.9 reduce-scatter.4
